TPU v7x, 32 devices: a whole 2x2x4 slice. The times are simulated.
32 devices in a mesh: expert: 4 (over y, core), mp: 2 (over x), dp: 4 (over z).
Axes of the slice: x: 2, y: 2, z: 4, core: 2. Of those that a mesh axis runs over, the one named last changes fastest.
Arguments:
- tokens: bfloat16 [256, 4096], P(('expert', 'dp'), 'mp'), may hold values from -6 to 6
- rotation: bfloat16 [4096, 4096], P('mp', ('expert', 'dp')), may hold values from -0.09375 to 0.09375
- expert_ids: int32 [256, 2], P(('expert', 'dp')), may hold values from 0 to 3, all different within a row; in each aligned block of 16 rows (0 to 15, 16 to 31, ...) at most 12 rows name the same one
- combine: float32 [256, 2], P(('expert', 'dp')), may hold values from 0.1 to 1
- w_gate: bfloat16 [4, 14336, 4096], P('expert', ('mp', 'dp')), may hold values from -0.09375 to 0.09375
- w_up: bfloat16 [4, 14336, 4096], P('expert', ('mp', 'dp')), may hold values from -0.09375 to 0.09375
- w_down: bfloat16 [4, 14336, 4096], P('expert', ('mp', 'dp')), may hold values from -0.046875 to 0.046875
- clip_scale: float32 [4, 14336], P('expert', ('mp', 'dp')), may hold values from 0.25 to 2
- cotangent: bfloat16 [256, 4096], P(('expert', 'dp'), 'mp'), may hold values from -2 to 2
Outputs:
- layer_out: bfloat16 [256, 4096], P(('expert', 'dp'), 'mp')
- rotation_grad: float32 [4096, 4096], P('mp', ('expert', 'dp'))
Inputs may be any that keep to these rules, and one draw needn't show every extreme that they name: `expert_ids`: each token names 2 different experts. In each aligned block of 16 tokens (the tokens of one index of expert and dp), no expert is named by more than 12 tokens, a bound that some block reaches.
All inputs are finite; a program needn't handle non-finite values.
Results may differ from a plain program's by a relative error of at most 0.0098.
Values may be sent and summed in bfloat16 or wider, within the bound.
A program may use at most 128 MiB of HBM per device.

v0:
```python
import math

import jax
import jax.numpy as jnp
from jax import lax
from jax.sharding import PartitionSpec as P

TOP = 2
HB = 64


def hadamard_table(block_size):
    bit_index = jnp.arange(block_size, dtype=jnp.int32)
    common_bits = jnp.bitwise_and(bit_index[:, None], bit_index[None, :])
    parity = jnp.zeros((block_size, block_size), jnp.int32)
    for bit_pos in range(block_size.bit_length() - 1):
        parity = parity + jnp.bitwise_and(jnp.right_shift(common_bits, bit_pos), 1)
    sign_table = 1 - 2 * (parity % 2)
    return sign_table.astype(jnp.float32) / math.sqrt(block_size)


def blocked(values, hadamard):
    row_count, col_count = values.shape
    block_size = hadamard.shape[0]
    blocks_view = values.reshape(row_count, col_count // block_size, block_size)
    mixed = jnp.einsum("rbk,kj->rbj", blocks_view, hadamard, precision=lax.Precision.HIGHEST)
    return mixed.reshape(row_count, col_count)


def pack_rows(routing, rows_in):
    packed = jnp.einsum(
        "ect,td->ecd", routing, rows_in.astype(jnp.float32), precision=lax.Precision.HIGHEST
    )
    return packed.astype(jnp.bfloat16)


def local(tokens, rotation, expert_ids, combine, w_gate, w_up, w_down, clip_scale, cotangent):
    n_expert = lax.axis_size("expert")
    n_model = lax.axis_size("mp")
    tok_rows, local_width = tokens.shape
    capacity = min(tok_rows, 3 * tok_rows * TOP // (2 * n_expert))
    model_idx = lax.axis_index("mp")
    token_all = lax.all_gather(tokens, ("expert", "dp"), axis=0, tiled=True)
    part_cols = jnp.dot(token_all, rotation, preferred_element_type=jnp.float32)
    summed_cols = lax.psum(part_cols, "mp").astype(jnp.bfloat16)
    rotated_wide = lax.all_to_all(
        summed_cols, ("expert", "dp"), split_axis=0, concat_axis=1, tiled=True
    )
    rotated = lax.dynamic_slice_in_dim(rotated_wide, model_idx * local_width, local_width, 1)
    labels = jnp.arange(n_expert, dtype=jnp.int32)
    expert_hits = expert_ids[:, :, None] == labels[None, None, :]
    member = jnp.any(expert_hits, axis=1).astype(jnp.int32)
    weight = jnp.sum(jnp.where(expert_hits, combine[:, :, None], 0.0), axis=1)
    slot_rank = jnp.cumsum(member, axis=0) - member
    slot_ids = jnp.arange(capacity, dtype=jnp.int32)
    routing = (
        (slot_rank[:, :, None] == slot_ids[None, None, :]) & (member[:, :, None] > 0)
    ).astype(jnp.float32)
    routing = jnp.transpose(routing, (1, 2, 0))
    weighted = routing * jnp.transpose(weight)[:, None, :]
    send_in = pack_rows(routing, rotated)
    send_cot = pack_rows(weighted, cotangent)
    recv_in, recv_cot = (
        lax.all_to_all(send_in, "expert", split_axis=0, concat_axis=0, tiled=True),
        lax.all_to_all(send_cot, "expert", split_axis=0, concat_axis=0, tiled=True),
    )
    recv_in = recv_in.reshape(n_expert * capacity, local_width)
    recv_cot = recv_cot.reshape(n_expert * capacity, local_width)
    recv_in, recv_cot = (
        lax.all_gather(recv_in, "mp", axis=1, tiled=True),
        lax.all_gather(recv_cot, "mp", axis=1, tiled=True),
    )
    expert_in, expert_cot = (
        lax.all_gather(recv_in, "dp", axis=0, tiled=True),
        lax.all_gather(recv_cot, "dp", axis=0, tiled=True),
    )
    gate_w = w_gate[0]
    up_w = w_up[0]
    down_w = w_down[0]
    clip_row = clip_scale[0]
    contract = (((1,), (1,)), ((), ()))
    total_rows = expert_in.shape[0]
    hadamard = hadamard_table(HB)
    gate_act = lax.dot_general(expert_in, gate_w, contract, preferred_element_type=jnp.float32)
    up_act = lax.dot_general(expert_in, up_w, contract, preferred_element_type=jnp.float32)
    gate_sig = jax.nn.sigmoid(gate_act)
    hidden = gate_act * gate_sig * up_act
    squash = jnp.tanh(blocked(hidden, hadamard) / clip_row)
    quant = (clip_row * squash).astype(jnp.bfloat16)
    down_three = down_w.reshape(down_w.shape[0], n_model, local_width)
    out_terms = jnp.einsum("rf,fmk->mrk", quant, down_three, preferred_element_type=jnp.float32)
    out_terms = out_terms.reshape(n_model * total_rows, local_width)
    expert_out = lax.psum_scatter(out_terms, ("mp", "dp"), scatter_dimension=0, tiled=True).astype(
        jnp.bfloat16
    )
    back_out = lax.all_to_all(
        expert_out.reshape(n_expert, capacity, local_width),
        "expert",
        split_axis=0,
        concat_axis=0,
        tiled=True,
    )
    layer_out = jnp.einsum(
        "ect,ecd->td", weighted, back_out.astype(jnp.float32), precision=lax.Precision.HIGHEST
    ).astype(jnp.bfloat16)
    d_quant = lax.dot_general(expert_cot, down_w, contract, preferred_element_type=jnp.float32)
    d_hidden = blocked(d_quant * (1.0 - squash * squash), hadamard)
    d_gate = (d_hidden * up_act * gate_sig * (1.0 + gate_act * (1.0 - gate_sig))).astype(
        jnp.bfloat16
    )
    d_up = (d_hidden * gate_act * gate_sig).astype(jnp.bfloat16)
    gate_three = gate_w.reshape(gate_w.shape[0], n_model, local_width)
    up_three = up_w.reshape(up_w.shape[0], n_model, local_width)
    grad_terms = jnp.einsum(
        "rf,fmk->mrk", d_gate, gate_three, preferred_element_type=jnp.float32
    ) + jnp.einsum("rf,fmk->mrk", d_up, up_three, preferred_element_type=jnp.float32)
    grad_terms = grad_terms.reshape(n_model * total_rows, local_width)
    expert_grad = lax.psum_scatter(
        grad_terms, ("mp", "dp"), scatter_dimension=0, tiled=True
    ).astype(jnp.bfloat16)
    back_grad = lax.all_to_all(
        expert_grad.reshape(n_expert, capacity, local_width),
        "expert",
        split_axis=0,
        concat_axis=0,
        tiled=True,
    )
    d_rotated = jnp.einsum(
        "ect,ecd->td", routing, back_grad.astype(jnp.float32), precision=lax.Precision.HIGHEST
    ).astype(jnp.bfloat16)
    wide_grad = lax.all_gather(d_rotated, "mp", axis=1, tiled=True)
    token_contract = (((0,), (0,)), ((), ()))
    grad_block = lax.all_to_all(
        wide_grad, ("expert", "dp"), split_axis=1, concat_axis=0, tiled=True
    )
    rotation_grad = lax.dot_general(
        token_all, grad_block, token_contract, preferred_element_type=jnp.float32
    )
    return (layer_out, rotation_grad)


def solution(mesh):
    return jax.shard_map(
        local,
        mesh=mesh,
        in_specs=(
            P(("expert", "dp"), "mp"),
            P("mp", ("expert", "dp")),
            P(("expert", "dp"), None),
            P(("expert", "dp"), None),
            P("expert", ("mp", "dp"), None),
            P("expert", ("mp", "dp"), None),
            P("expert", ("mp", "dp"), None),
            P("expert", ("mp", "dp")),
            P(("expert", "dp"), "mp"),
        ),
        out_specs=(P(("expert", "dp"), "mp"), P("mp", ("expert", "dp"))),
        check_vma=False,
    )
```

profile of v0, /device:TPU:0, one launch (start us, length us, event | category | flops | bytes accessed | tf_op | source)
XLA Modules:
  0.0 433.9 jit_solution(6628575716274499822)
XLA Ops:
  8.7 42.1 %all-gather.4.cloned.1.call-done = bf16[256,2048]{1,0:T(8,128)(2,1)} async-done(((bf16[16,2048]{1,0:T(8,128)(2,1)}), bf16[256,2048]{1,0:T(8,128)(2,1)}) %all-gather.4.cloned.1.call-update) | async-done | bytes 1048592 | tf_op jit(solution)/shard_map/all_gather | solution.py:43
  52.5 12.6 %all-reduce.1 = bf16[256,256]{1,0:T(8,128)(2,1)} all-reduce(f32[256,256]{1,0:T(8,128)S(1)} %fusion.88), channel_id=1, replica_groups=mesh['expert'=4,'mp'=2,'dp'=4] {'mp'}, use_global_device_ids=true, to_apply=%region_3.4 | all-reduce | flops 65536 | bytes 393216 | tf_op jit(solution)/shard_map/psum | solution.py:45
  65.1 3.7 all-to-all-start
  69.1 7.1 %all-to-all-done = bf16[16,16,256]{2,1,0:T(8,128)(2,1)S(1)} async-done(((bf16[16,16,256]{2,1,0:T(8,128)(2,1)}), bf16[16,16,256]{2,1,0:T(8,128)(2,1)S(1)}, u32[]{:S(2)}, u32[]{:S(2)}) %all-to-all-start) | async-done | bytes 131104 | tf_op jit(solution)/shard_map/all_to_all | solution.py:46
  76.6 8.4 %all_to_all.58 = bf16[4,12,2048]{2,1,0:T(8,128)(2,1)S(1)} all-to-all(bf16[4,12,2048]{2,1,0:T(8,128)(2,1)S(1)} %convolution_convert_fusion.1), channel_id=1, replica_groups=mesh['expert'=4,'mp'=2,'dp'=4] {'expert'}, dimensions={0} | all-to-all | bytes 393216 | tf_op jit(solution)/shard_map/all_to_all | solution.py:64
  85.0 7.0 %all_gather.19 = bf16[48,4096]{1,0:T(8,128)(2,1)} all-gather(bf16[48,2048]{1,0:T(8,128)(2,1)S(1)} %reshape.70), channel_id=1, replica_groups=mesh['expert'=4,'mp'=2,'dp'=4] {'mp'}, dimensions={1}, use_global_device_ids=true | all-gather | bytes 589824 | tf_op jit(solution)/shard_map/all_gather | solution.py:70
  93.3 3.4 all-to-all-start.3
  96.9 24.6 %reshape_squeeze.11 = bf16[1792,2,2048]{2,1,0:T(2,128)(2,1)} reshape(bf16[1,1792,4096]{2,1,0:T(8,128)(2,1)} %param.14) | data formatting | bytes 29360128 | tf_op jit(solution)/shard_map/reshape;squeeze | solution.py:113
  121.5 24.4 %reshape_squeeze.10 = bf16[1792,2,2048]{2,1,0:T(2,128)(2,1)} reshape(bf16[1,1792,4096]{2,1,0:T(8,128)(2,1)} %param.13) | data formatting | bytes 29360128 | tf_op jit(solution)/shard_map/reshape;squeeze | solution.py:112
  146.0 8.0 %all_gather.21 = bf16[48,4096]{1,0:T(8,128)(2,1)} all-gather(bf16[48,2048]{1,0:T(8,128)(2,1)S(1)} %reshape.74), channel_id=1, replica_groups=mesh['expert'=4,'mp'=2,'dp'=4] {'mp'}, dimensions={1}, use_global_device_ids=true | all-gather | bytes 589824 | tf_op jit(solution)/shard_map/all_gather | solution.py:71
  154.5 8.8 %fusion.4 = f32[192,1792]{1,0:T(8,128)S(1)} fusion(bf16[192,4096]{1,0:T(8,128)(2,1)} %all-gather.6.cloned.1.call-done, bf16[1,1792,4096]{2,1,0:T(8,128)(2,1)} %param.13), kind=kOutput, calls=%fused_computation.4 | convolution fusion | flops 2818572288 | bytes 17629184 | tf_op jit(solution)/shard_map/dot_general | solution.py:84
  163.3 12.3 %multiply_multiply_fusion = (f32[192,1792]{1,0:T(8,128)}, f32[192,1792]{1,0:T(8,128)}) fusion(f32[192,1792]{1,0:T(8,128)S(1)} %fusion.4, bf16[192,4096]{1,0:T(8,128)(2,1)S(1)} %copy-done.6, bf16[1,1792,4096]{2,1,0:T(8,128)(2,1)} %param.14), kind=kOutput, calls=%fused_computation.24 | convolution fusion | flops 2820292608 | bytes 20381696 | tf_op jit(solution)/shard_map/dot_general | solution.py:85
  177.3 3.8 multiply_convert_fusion
  181.2 1.8 copy.54
  182.9 6.1 %all-gather.8.cloned.1.call-done = bf16[192,4096]{1,0:T(8,128)(2,1)} async-done(((bf16[48,4096]{1,0:T(8,128)(2,1)}), bf16[192,4096]{1,0:T(8,128)(2,1)}) %all-gather.8.cloned.1.call-update) | async-done | bytes 1572880 | tf_op jit(solution)/shard_map/all_gather | solution.py:75
  189.0 11.7 %fusion.15 = f32[192,1792]{1,0:T(8,128)} fusion(bf16[192,4096]{1,0:T(8,128)(2,1)} %all-gather.8.cloned.1.call-done, bf16[1,1792,4096]{2,1,0:T(8,128)(2,1)} %param.15, f32[192,1792]{1,0:T(8,128)S(1)} %copy.54, f32[1792]{0:T(1024)S(1)} %reduce), kind=kOutput, calls=%fused_computation.14 | convolution fusion | flops 2819948544 | bytes 19012608 | tf_op jit(solution)/shard_map/dot_general | solution.py:106
  200.8 12.5 %copy.55 = f32[192,1792]{0,1:T(8,128)S(1)} copy(f32[192,1792]{1,0:T(8,128)} %fusion.15) | data formatting | bytes 2752512 | tf_op jit(solution)/shard_map/mul | solution.py:107
  213.2 3.1 fusion.38
  216.3 2.8 copy.56
  219.1 17.3 %fusion.6 = f32[192,2,2048]{2,0,1:T(8,128)} fusion(bf16[1792,2,2048]{2,1,0:T(2,128)(2,1)} %reshape_squeeze.11, f32[192,1792]{1,0:T(8,128)} %copy.56, f32[192,1792]{1,0:T(8,128)} %copy-done.8), kind=kOutput, calls=%fused_computation.6 | convolution fusion | flops 2820636672 | bytes 20578304 | tf_op jit(solution)/shard_map/rf,fmk->mrk/dot_general | solution.py:116
  236.4 13.9 %fusion.12 = f32[192,2,2048]{2,0,1:T(8,128)} fusion(f32[192,2,2048]{2,0,1:T(8,128)} %fusion.6, bf16[1792,2,2048]{2,1,0:T(2,128)(2,1)S(1)} %bitcast.83, f32[192,1792]{1,0:T(8,128)} %copy-done.8, f32[192,1792]{1,0:T(8,128)} %copy.56, f32[192,1792]{1,0:T(8,128)} %get-tuple-element.11), kind=kOutput, calls=%fused_computation.12 | convolution fusion | flops 2822799360 | bytes 25100288 | tf_op jit(solution)/shard_map/rf,fmk->mrk/dot_general | solution.py:114
  250.4 24.8 %reshape_squeeze.9 = bf16[1792,2,2048]{2,1,0:T(2,128)(2,1)} reshape(bf16[1,1792,4096]{2,1,0:T(8,128)(2,1)} %param.15) | data formatting | bytes 29360128 | tf_op jit(solution)/shard_map/reshape;squeeze | solution.py:90
  275.2 16.2 %fusion.10 = f32[192,2,2048]{2,0,1:T(8,128)} fusion(bf16[192,1792,1]{0,1,2:T(8,128)(2,1)S(1)} %bitcast.96, bf16[1792,2,2048]{2,1,0:T(2,128)(2,1)} %reshape_squeeze.9), kind=kOutput, calls=%fused_computation.10 | convolution fusion | flops 2818572288 | bytes 18513920 | tf_op jit(solution)/shard_map/rf,fmk->mrk/dot_general | solution.py:91
  291.5 32.0 %reduce-scatter.5.cloned.1.call-done = f32[48,2048]{1,0:T(8,128)} async-done(((f32[384,2048]{1,0:T(8,128)}), f32[48,2048]{1,0:T(8,128)}) %reduce-scatter.5.cloned.1.call-update) | async-done | bytes 393232 | tf_op jit(solution)/shard_map/reduce_scatter | solution.py:118
  325.3 3.4 all-to-all-start.4
  328.7 71.8 %reduce-scatter.3.cloned.1.call-done = f32[48,2048]{1,0:T(8,128)} async-done(((f32[384,2048]{1,0:T(8,128)}), f32[48,2048]{1,0:T(8,128)}) %reduce-scatter.3.cloned.1.call-update) | async-done | bytes 393232 | tf_op jit(solution)/shard_map/reduce_scatter | solution.py:93
  402.3 3.4 all-to-all-start.2
  406.0 5.1 %all_gather.23 = bf16[16,4096]{1,0:T(8,128)(2,1)S(1)} all-gather(bf16[16,2048]{1,0:T(8,128)(2,1)S(1)} %fusion.19), channel_id=1, replica_groups=mesh['expert'=4,'mp'=2,'dp'=4] {'mp'}, dimensions={1}, use_global_device_ids=true | all-gather | bytes 196608 | tf_op jit(solution)/shard_map/all_gather | solution.py:131
  411.8 4.3 %all-to-all-start.5 = ((bf16[16,16,256]{2,0,1:T(8,128)(2,1)}), bf16[16,16,256]{2,0,1:T(8,128)(2,1)S(1)}, u32[]{:S(2)}, u32[]{:S(2)}) async-start(bf16[16,16,256]{2,0,1:T(8,128)(2,1)} %bitcast.81), calls=%async_computation.7 | async-start | bytes 262144 | tf_op jit(solution)/shard_map/all_to_all | solution.py:133
  417.3 6.2 %all-to-all-done.5 = bf16[16,16,256]{2,0,1:T(8,128)(2,1)S(1)} async-done(((bf16[16,16,256]{2,0,1:T(8,128)(2,1)}), bf16[16,16,256]{2,0,1:T(8,128)(2,1)S(1)}, u32[]{:S(2)}, u32[]{:S(2)}) %all-to-all-start.5) | async-done | bytes 131104 | tf_op jit(solution)/shard_map/all_to_all | solution.py:133
  423.5 1.8 convolution_bitcast_fusion
  425.3 1.8 copy.61
  (65 shorter events, 13.2 us)
Async XLA Ops:
  7.2 43.7 %copy-start = (bf16[2048,256]{1,0:T(8,128)(2,1)S(1)}, bf16[2048,256]{1,0:T(8,128)(2,1)}, u32[]{:S(2)}) copy-start(bf16[2048,256]{1,0:T(8,128)(2,1)} %param.10) | copy-start | bytes 3145732
  7.2 43.6 %all-gather.4.cloned.1.call-start = ((), (), s32[]{:S(2)}) async-start(), calls=%async_computation.8 | async-start | bytes 1114112 | tf_op jit(solution)/shard_map/all_gather | solution.py:43
  52.5 39.6 %copy-start.4 = (s32[16,2]{0,1:T(2,128)S(1)}, s32[16,2]{0,1:T(2,128)}, u32[]{:S(2)}) copy-start(s32[16,2]{0,1:T(2,128)} %param.11) | copy-start | bytes 388
  52.5 39.6 %copy-start.5 = (f32[16,2]{0,1:T(2,128)S(1)}, f32[16,2]{0,1:T(2,128)}, u32[]{:S(2)}) copy-start(f32[16,2]{0,1:T(2,128)} %param.12) | copy-start | bytes 388
  52.5 39.6 %copy-start.2 = (bf16[16,2048]{1,0:T(8,128)(2,1)S(1)}, bf16[16,2048]{1,0:T(8,128)(2,1)}, u32[]{:S(2)}) copy-start(bf16[16,2048]{1,0:T(8,128)(2,1)} %param.17) | copy-start | bytes 196612
  65.1 11.1 %all-to-all-start = ((bf16[16,16,256]{2,1,0:T(8,128)(2,1)}), bf16[16,16,256]{2,1,0:T(8,128)(2,1)S(1)}, u32[]{:S(2)}, u32[]{:S(2)}) async-start(bf16[16,16,256]{2,1,0:T(8,128)(2,1)} %bitcast.3), calls=%async_computation | async-start | bytes 262144 | tf_op jit(solution)/shard_map/all_to_all | solution.py:46
  68.8 85.6 %all-gather.6.cloned.1.call-start = ((), (), s32[]{:S(2)}) async-start(), calls=%async_computation.9 | async-start | bytes 1966080 | tf_op jit(solution)/shard_map/all_gather | solution.py:74
  76.2 20.6 %copy-start.3 = (f32[1,1792]{1,0:T(1,128)S(1)}, f32[1,1792]{1,0:T(1,128)}, u32[]{:S(2)}) copy-start(f32[1,1792]{1,0:T(1,128)} %param.16) | copy-start | bytes 21508
  93.3 52.6 %all-to-all-start.3 = ((bf16[4,12,2048]{2,1,0:T(8,128)(2,1)}), bf16[4,12,2048]{2,1,0:T(8,128)(2,1)S(1)}, u32[]{:S(2)}, u32[]{:S(2)}) async-start(bf16[4,12,2048]{2,1,0:T(8,128)(2,1)} %convolution_convert_fusion), calls=%async_computation.4 | async-start | bytes 524288 | tf_op jit(solution)/shard_map/all_to_all | solution.py:65
  96.8 92.3 %all-gather.8.cloned.1.call-start = ((), (), s32[]{:S(2)}) async-start(), calls=%async_computation.11 | async-start | bytes 1966080 | tf_op jit(solution)/shard_map/all_gather | solution.py:75
  154.0 169.5 %reduce-scatter.5.cloned.1.call-start = ((), (), s32[]{:S(2)}) async-start(), calls=%async_computation.12 | async-start | bytes 3538944 | tf_op jit(solution)/shard_map/reduce_scatter | solution.py:118
  154.5 8.8 %copy-start.6 = (bf16[192,4096]{1,0:T(8,128)(2,1)S(1)}, bf16[192,4096]{1,0:T(8,128)(2,1)}, u32[]{:S(2)}) copy-start(bf16[192,4096]{1,0:T(8,128)(2,1)} %all-gather.6.cloned.1.call-done) | copy-start | bytes 4718596
  163.3 12.3 %copy-start.8 = (f32[192,1792]{1,0:T(8,128)}, f32[192,1792]{1,0:T(8,128)S(1)}, u32[]{:S(2)}) copy-start(f32[192,1792]{1,0:T(8,128)S(1)} %fusion.4) | copy-start | bytes 4128772
  216.3 20.1 %slice-start = ((s8[14680064]{0:T(1024)(128)(4,1)}), s8[2097152]{0:T(1024)(128)(4,1)S(1)}, s32[]{:S(2)}) async-start(s8[14680064]{0:T(1024)(128)(4,1)} %bitcast.82), calls=%async_computation.13 | async-start | bytes 4194304
  219.1 17.3 %slice-start.1 = ((s8[14680064]{0:T(1024)(128)(4,1)}), s8[4194304]{0:T(1024)(128)(4,1)S(1)}, s32[]{:S(2)}) async-start(s8[14680064]{0:T(1024)(128)(4,1)} %bitcast.82), calls=%async_computation.14 | async-start | bytes 8388608
  219.1 17.3 %slice-start.2 = ((s8[14680064]{0:T(1024)(128)(4,1)}), s8[4194304]{0:T(1024)(128)(4,1)S(1)}, s32[]{:S(2)}) async-start(s8[14680064]{0:T(1024)(128)(4,1)} %bitcast.82), calls=%async_computation.15 | async-start | bytes 8388608
  219.1 17.3 %slice-start.3 = ((s8[14680064]{0:T(1024)(128)(4,1)}), s8[4194304]{0:T(1024)(128)(4,1)S(1)}, s32[]{:S(2)}) async-start(s8[14680064]{0:T(1024)(128)(4,1)} %bitcast.82), calls=%async_computation.16 | async-start | bytes 8388608
  250.3 24.9 %copy-start.7 = (bf16[192,28,64]{0,2,1:T(8,128)(2,1)S(1)}, bf16[192,28,64]{0,2,1:T(8,128)(2,1)}, u32[]{:S(2)}) copy-start(bf16[192,28,64]{0,2,1:T(8,128)(2,1)} %get-tuple-element.12) | copy-start | bytes 2064388
  250.4 150.2 %reduce-scatter.3.cloned.1.call-start = ((), (), s32[]{:S(2)}) async-start(), calls=%async_computation.10 | async-start | bytes 3538944 | tf_op jit(solution)/shard_map/reduce_scatter | solution.py:93
  325.3 77.0 %all-to-all-start.4 = ((bf16[4,12,2048]{2,1,0:T(8,128)(2,1)}), bf16[4,12,2048]{2,1,0:T(8,128)(2,1)S(1)}, u32[]{:S(2)}, u32[]{:S(2)}) async-start(bf16[4,12,2048]{2,1,0:T(8,128)(2,1)} %reshape.79), calls=%async_computation.6 | async-start | bytes 524288 | tf_op jit(solution)/shard_map/all_to_all | solution.py:121
  402.3 9.5 %all-to-all-start.2 = ((bf16[4,12,2048]{2,1,0:T(8,128)(2,1)}), bf16[4,12,2048]{2,1,0:T(8,128)(2,1)S(1)}, u32[]{:S(2)}, u32[]{:S(2)}) async-start(bf16[4,12,2048]{2,1,0:T(8,128)(2,1)} %reshape.73), calls=%async_computation.3 | async-start | bytes 524288 | tf_op jit(solution)/shard_map/all_to_all | solution.py:96
  411.8 11.7 %all-to-all-start.5 = ((bf16[16,16,256]{2,0,1:T(8,128)(2,1)}), bf16[16,16,256]{2,0,1:T(8,128)(2,1)S(1)}, u32[]{:S(2)}, u32[]{:S(2)}) async-start(bf16[16,16,256]{2,0,1:T(8,128)(2,1)} %bitcast.81), calls=%async_computation.7 | async-start | bytes 262144 | tf_op jit(solution)/shard_map/all_to_all | solution.py:133
  423.5 3.6 copy-start.1
Sparse Core Ops, SparseCore 0:
  10.2 40.5 all-gather.3
  92.2 34.1 all-gather.5
  154.1 34.8 all-gather.7
  250.5 73.0 reduce-scatter.4
  327.0 73.4 reduce-scatter.2
where the time goes:
time: 434 us
  waiting for transfers between devices  166 us (38%)
  local copies, waits for them, and re-layouts  97.1 us (22%)
  matrix products  93.5 us (22%)
  blocking collectives  41.2 us (9%)
  starting transfers between devices  18.8 us (4%)
  between operations  14.3 us (3%)
    reduce_scatter x1, waiting for transfers between devices, local(): lax.psum_scatter(out_terms, ('mp', 'dp'), scatter_dimension=0, tiled=True)  71.8 us
    all_gather x1, waiting for transfers between devices, local(): token_all = lax.all_gather(tokens, ('expert', 'dp'), axis=0, tiled=True)  42.1 us
    reduce_scatter x1, waiting for transfers between devices, local(): lax.psum_scatter(grad_terms, ('mp', 'dp'), scatter_dimension=0, tiled=True)  32 us
    another operation x1, local copies, waits for them, and re-layouts, local(): down_three = down_w.reshape(down_w.shape[0], n_model, local_width)  24.8 us
    another operation x1, local copies, waits for them, and re-layouts, local(): up_three = up_w.reshape(up_w.shape[0], n_model, local_width)  24.6 us
    another operation x1, local copies, waits for them, and re-layouts, local(): gate_three = gate_w.reshape(gate_w.shape[0], n_model, local_width)  24.4 us
    dot_general x1, matrix products, local(): jnp.einsum('rf,fmk->mrk', d_up, up_three, preferred_element_type=jnp.floa...  17.3 us
    dot_general x1, matrix products, local(): jnp.einsum('rf,fmk->mrk', quant, down_three, preferred_element_type=jnp.f...  16.2 us
  transfers between devices with their start and end apart: 10, of which 6 were waited for; matrix products, arithmetic and copies ran while one was open for 29% of the time, Pallas kernels for 0%

commit v1 on v0

v1 whole, which is shorter than its diff:
```python
import functools
import math

import jax
import jax.numpy as jnp
import numpy as np
from jax import lax
from jax.experimental import pallas as pl
from jax.experimental.pallas import tpu as pltpu
from jax.sharding import PartitionSpec as P

HB = 64


def sign_table(width):
    row = lax.broadcasted_iota(jnp.int32, (width, width), 0)
    col = lax.broadcasted_iota(jnp.int32, (width, width), 1)
    common = jnp.bitwise_and(jnp.bitwise_and(row, col), HB - 1)
    parity = jnp.zeros((width, width), jnp.int32)
    for bit_pos in range(HB.bit_length() - 1):
        parity = parity + jnp.bitwise_and(jnp.right_shift(common, bit_pos), 1)
    sign = (1 - 2 * jnp.bitwise_and(parity, 1)).astype(jnp.float32)
    same = jnp.right_shift(row, HB.bit_length() - 1) == jnp.right_shift(col, HB.bit_length() - 1)
    return jnp.where(same, sign, 0.0).astype(jnp.bfloat16)


def mix(values, table):
    high = values.astype(jnp.bfloat16)
    low = (values - high.astype(jnp.float32)).astype(jnp.bfloat16)
    total = jnp.dot(high, table, preferred_element_type=jnp.float32)
    total = total + jnp.dot(low, table, preferred_element_type=jnp.float32)
    return total * (1.0 / math.sqrt(HB))


NT = (((1,), (1,)), ((), ()))


def expert_kernel(x_ref, c_ref, w_ref, clip_ref, table_ref, gw_ref, uw_ref, dw_ref, out_ref, grad_ref):
    step = pl.program_id(0)

    @pl.when(step == 0)
    def _():
        out_ref[...] = jnp.zeros_like(out_ref)
        grad_ref[...] = jnp.zeros_like(grad_ref)

    table = table_ref[...]
    clip = clip_ref[0]
    x = x_ref[...]
    gate_act = lax.dot_general(x, gw_ref[...], NT, preferred_element_type=jnp.float32)
    up_act = lax.dot_general(x, uw_ref[...], NT, preferred_element_type=jnp.float32)
    d_quant = lax.dot_general(c_ref[...], dw_ref[...], NT, preferred_element_type=jnp.float32)
    gate_sig = jax.nn.sigmoid(gate_act)
    silu = gate_act * gate_sig
    squash = jnp.tanh(mix(silu * up_act, table) / clip)
    quant = (clip * squash).astype(jnp.bfloat16)
    d_hidden = mix(d_quant * (1.0 - squash * squash), table)
    d_gate = (d_hidden * up_act * gate_sig * (1.0 + gate_act * (1.0 - gate_sig))).astype(jnp.bfloat16)
    d_up = (d_hidden * silu).astype(jnp.bfloat16)
    weight = w_ref[...]
    width = out_ref.shape[1]
    chunk = 512 if width % 512 == 0 else width

    @pl.loop(0, width // chunk)
    def _(i):
        cols = pl.ds(pl.multiple_of(i * chunk, chunk), chunk)
        out_ref[:, cols] += weight * jnp.dot(quant, dw_ref[:, cols], preferred_element_type=jnp.float32)
        grad_ref[:, cols] += jnp.dot(d_gate, gw_ref[:, cols], preferred_element_type=jnp.float32) + jnp.dot(
            d_up, uw_ref[:, cols], preferred_element_type=jnp.float32
        )


def expert_ffn(x, c, weight, clip, gate_w, up_w, down_w):
    rows, width = x.shape
    hidden = gate_w.shape[0]
    block = max(b for b in range(HB, 257, HB) if hidden % b == 0)
    steps = hidden // block
    table = sign_table(block)
    whole = lambda shape: pl.BlockSpec(shape, lambda s: (0,) * len(shape), pipeline_mode=pl.Buffered(1))
    wspec = pl.BlockSpec((block, width), lambda s: (s, 0))
    return pl.pallas_call(
        expert_kernel,
        grid=(steps,),
        in_specs=[
            whole((rows, width)),
            whole((rows, width)),
            whole((rows, 1)),
            pl.BlockSpec((1, 1, block), lambda s: (s, 0, 0)),
            whole((block, block)),
            wspec,
            wspec,
            wspec,
        ],
        out_specs=[pl.BlockSpec((rows, width), lambda s: (0, 0), pipeline_mode=pl.Buffered(1))] * 2,
        out_shape=[jax.ShapeDtypeStruct((rows, width), jnp.float32)] * 2,
        compiler_params=pltpu.CompilerParams(vmem_limit_bytes=60 * 1024 * 1024),
        cost_estimate=pl.CostEstimate(
            flops=12 * rows * hidden * width, bytes_accessed=6 * hidden * width, transcendentals=2 * rows * hidden
        ),
    )(x, c, weight, clip.reshape(steps, 1, block), table, gate_w, up_w, down_w)


def local(tokens, rotation, expert_ids, combine, w_gate, w_up, w_down, clip_scale, cotangent):
    n_expert = lax.axis_size("expert")
    tok_axes = ("expert", "dp")
    labels = jnp.arange(n_expert, dtype=jnp.int32)
    hits = expert_ids[:, :, None] == labels[None, None, :]
    weight = jnp.sum(jnp.where(hits, combine[:, :, None], 0.0), axis=1)
    token_all = lax.all_gather(tokens, tok_axes, axis=0, tiled=True)
    part_cols = jnp.dot(token_all, rotation, preferred_element_type=jnp.float32)
    block_cols = lax.psum(part_cols, "mp").astype(jnp.bfloat16)
    rotated = lax.all_gather(block_cols, tok_axes, axis=1, tiled=True)
    weight_all = lax.all_gather(weight, tok_axes, axis=0, tiled=True)
    mine = lax.dynamic_slice_in_dim(weight_all, lax.axis_index("expert"), 1, 1)
    cot_half = lax.all_gather(cotangent, "mp", axis=1, tiled=True)
    cot_all = lax.all_gather(cot_half, tok_axes, axis=0, tiled=True)
    expert_cot = (mine * cot_all.astype(jnp.float32)).astype(jnp.bfloat16)
    out_part, grad_part = expert_ffn(
        rotated, expert_cot, mine, clip_scale[0], w_gate[0], w_up[0], w_down[0]
    )
    out_rows = lax.psum_scatter(out_part, tok_axes, scatter_dimension=0, tiled=True)
    layer_out = lax.psum_scatter(out_rows, "mp", scatter_dimension=1, tiled=True).astype(jnp.bfloat16)
    grad_cols = lax.psum_scatter(grad_part, tok_axes, scatter_dimension=1, tiled=True)
    d_rotated = lax.psum(grad_cols, "mp").astype(jnp.bfloat16)
    rotation_grad = lax.dot_general(
        token_all, d_rotated, (((0,), (0,)), ((), ())), preferred_element_type=jnp.float32
    )
    return (layer_out, rotation_grad)


def solution(mesh):
    return jax.shard_map(
        local,
        mesh=mesh,
        in_specs=(
            P(("expert", "dp"), "mp"),
            P("mp", ("expert", "dp")),
            P(("expert", "dp"), None),
            P(("expert", "dp"), None),
            P("expert", ("mp", "dp"), None),
            P("expert", ("mp", "dp"), None),
            P("expert", ("mp", "dp"), None),
            P("expert", ("mp", "dp")),
            P(("expert", "dp"), "mp"),
        ),
        out_specs=(P(("expert", "dp"), "mp"), P("mp", ("expert", "dp"))),
        check_vma=False,
    )
```

time: 434 us -> 355 us (0.82)
  local copies, waits for them, and re-layouts: 97.1 us -> 2.75 us
  matrix products: 93.5 us -> 3.34 us
  waiting for transfers between devices: 166 us -> 218 us
  Pallas kernels: 0 us -> 45.2 us
  blocking collectives: 41.2 us -> 64.1 us
  starting transfers between devices: 18.8 us -> 0.24 us
    dot_general x13 -> x1, matrix products: 91.9 us -> 1.68 us  [local(): lax.dot_general(token_all, d_rotated, (((0,), (0,)), ((), ())), preferred...]
    another operation x3 -> x0, local copies, waits for them, and re-layouts: 73.8 us -> none  [the longest x1 24.8 us: local(): down_three = down_w.reshape(down_w.shape[0], n_model, local_width)]
    pallas_call x0 -> x1, Pallas kernels: none -> 45.2 us  [expert_ffn(): pl.pallas_call(expert_kernel, grid=(steps,), in_specs=[whole((rows, width...]
    reduce_scatter x2 -> x3, waiting for transfers between devices: 104 us -> 147 us  [the longest x1 75.6 us: local(): lax.psum_scatter(grad_part, tok_axes, scatter_dimension=1, tiled=True)]
    all_gather x3, waiting for transfers between devices: 48.2 us -> 69.7 us  [the longest x1 35.1 us: local(): token_all = lax.all_gather(tokens, tok_axes, axis=0, tiled=True)]
    all_to_all x5 -> x0, starting transfers between devices: 18.3 us -> none  [the longest x1 4.34 us: local(): lax.all_to_all(wide_grad, ('expert', 'dp'), split_axis=1, concat_axis=0,...]
    all_gather x3 -> x2, blocking collectives: 20.2 us -> 37.5 us  [the longest x1 29.8 us: local(): weight_all = lax.all_gather(weight, tok_axes, axis=0, tiled=True)]
    mul x3 -> x0, local copies, waits for them, and re-layouts: 14.3 us -> none  [the longest x1 12.5 us: local(): d_hidden = blocked(d_quant * (1.0 - squash * squash), hadamard)]
  transfers between devices with their start and end apart: 10 -> 6, of which waited for: 6 -> 4; matrix products, arithmetic and copies ran while one was open for 29% -> 3% of each run, Pallas kernels for 0% -> 0%
where the time goes in v1:
time: 355 us; the launch traced here: 354 us
  waiting for transfers between devices  218 us (61%)
  blocking collectives  64.1 us (18%)
  Pallas kernels  45.2 us (13%)
  between operations  14.1 us (4%)
  other arithmetic  6.63 us (2%)
    reduce_scatter x1, waiting for transfers between devices, local(): lax.psum_scatter(grad_part, tok_axes, scatter_dimension=1, tiled=True)  75.6 us
    reduce_scatter x1, waiting for transfers between devices, local(): lax.psum_scatter(out_part, tok_axes, scatter_dimension=0, tiled=True)  71.4 us
    pallas_call x1, Pallas kernels, expert_ffn(): pl.pallas_call(expert_kernel, grid=(steps,), in_specs=[whole((rows, width...  45.2 us
    all_gather x1, waiting for transfers between devices, local(): token_all = lax.all_gather(tokens, tok_axes, axis=0, tiled=True)  35.1 us
    all_gather x1, waiting for transfers between devices, local(): rotated = lax.all_gather(block_cols, tok_axes, axis=1, tiled=True)  34.5 us
    all_gather x1, blocking collectives, local(): weight_all = lax.all_gather(weight, tok_axes, axis=0, tiled=True)  29.8 us
    psum x1, blocking collectives, local(): d_rotated = lax.psum(grad_cols, 'mp').astype(jnp.bfloat16)  14.2 us
    psum x1, blocking collectives, local(): block_cols = lax.psum(part_cols, 'mp').astype(jnp.bfloat16)  12.5 us
  transfers between devices with their start and end apart: 6, of which 4 were waited for; matrix products, arithmetic and copies ran while one was open for 3% of the time, Pallas kernels for 0%

profile of v1, /device:TPU:0, one launch (start us, length us, event | category | flops | bytes accessed | tf_op | source)
XLA Modules:
  0.0 354.3 jit_solution(8690589763109604534)
XLA Ops:
  7.2 0.0 copy-start
  7.2 0.0 all-gather.5.cloned.1.call-start
  7.2 0.7 all-gather.5.cloned.1.call-update
  7.9 0.0 all-gather.9.cloned.1.call-start
  8.0 7.6 %all_gather.18 = bf16[16,4096]{1,0:T(8,128)(2,1)} all-gather(bf16[16,2048]{1,0:T(8,128)(2,1)} %param.17), channel_id=1, replica_groups=mesh['expert'=4,'mp'=2,'dp'=4] {'mp'}, dimensions={1}, use_global_device_ids=true | all-gather | bytes 196608 | tf_op jit(solution)/shard_map/all_gather | solution.py:114
  15.6 0.0 all-gather.9.cloned.1.call-update
  15.6 0.0 all-gather.7.cloned.1.call-start
  15.7 35.1 %all-gather.5.cloned.1.call-done = bf16[256,2048]{1,0:T(8,128)(2,1)} async-done(((bf16[16,2048]{1,0:T(8,128)(2,1)}), bf16[256,2048]{1,0:T(8,128)(2,1)}) %all-gather.5.cloned.1.call-update) | async-done | bytes 1048592 | tf_op jit(solution)/shard_map/all_gather | solution.py:108
  50.8 0.0 copy-done
  50.8 1.7 fusion.2
  52.5 12.5 %all-reduce.2 = bf16[256,256]{1,0:T(8,128)(2,1)} all-reduce(f32[256,256]{1,0:T(8,128)S(1)} %fusion.2), channel_id=1, replica_groups=mesh['expert'=4,'mp'=2,'dp'=4] {'mp'}, use_global_device_ids=true, to_apply=%region_0.1 | all-reduce | flops 65536 | bytes 393216 | tf_op jit(solution)/shard_map/psum | solution.py:110
  65.0 0.0 all-gather.7.cloned.1.call-update
  65.0 0.0 reduce-scatter.4.cloned.1.call-start
  65.0 0.7 select_reduce_fusion
  65.8 29.8 %all-gather = f32[16,16,4]{1,2,0:T(4,128)S(1)} all-gather(f32[1,16,4]{1,2,0:T(4,128)S(1)} %bitcast.13), channel_id=1, replica_groups=mesh['expert'=4,'mp'=2,'dp'=4] {'expert','dp'}, dimensions={0}, use_global_device_ids=true | all-gather | bytes 4352 | tf_op jit(solution)/shard_map/all_gather | solution.py:112
  95.6 0.2 copy.23
  95.7 0.8 fusion.1
  96.5 0.9 select_convert_fusion.table_ref
  97.4 3.5 multiply_convert_fusion.c_ref
  100.9 34.5 %all-gather.7.cloned.1.call-done.x_ref = bf16[256,4096]{1,0:T(8,128)(2,1)} async-done(((bf16[256,256]{1,0:T(8,128)(2,1)}), bf16[256,4096]{1,0:T(8,128)(2,1)}) %all-gather.7.cloned.1.call-update) | async-done | bytes 2097168 | tf_op jit(solution)/shard_map/all_gather | solution.py:111
  135.4 45.2 %shard_map.104 = (f32[256,4096]{1,0:T(8,128)}, f32[256,4096]{1,0:T(8,128)}) custom-call(bf16[256,4096]{1,0:T(8,128)(2,1)} %all-gather.7.cloned.1.call-done.x_ref, bf16[256,4096]{1,0:T(8,128)(2,1)} %multiply_convert_fusion.c_ref, f32[256,1]{1,0:T(8,128)} %get-tuple-element.15.w_ref, f32[7,1,256]{2,1,0:T(1,128)} %bitcast.17, ...), custom_call_target="tpu_custom_call" | custom-call | flops 22548578304 | bytes 44040192 | tf_op jit(solution)/shard_map/pallas_call | solution.py:80
  180.6 0.0 reduce-scatter.4.cloned.1.call-update
  180.6 0.0 reduce-scatter.8.cloned.1.call-start
  180.6 0.5 reduce-scatter.8.cloned.1.call-update
  181.2 0.0 reduce-scatter.6.cloned.1.call-start
  181.2 71.4 %reduce-scatter.4.cloned.1.call-done = f32[16,4096]{1,0:T(8,128)} async-done(((f32[256,4096]{1,0:T(8,128)}), f32[16,4096]{1,0:T(8,128)}) %reduce-scatter.4.cloned.1.call-update) | async-done | bytes 262160 | tf_op jit(solution)/shard_map/reduce_scatter | solution.py:120
  252.6 0.0 reduce-scatter.6.cloned.1.call-update
  252.6 75.6 %reduce-scatter.8.cloned.1.call-done = f32[256,256]{1,0:T(8,128)} async-done(((f32[256,4096]{1,0:T(8,128)}), f32[256,256]{1,0:T(8,128)}) %reduce-scatter.8.cloned.1.call-update) | async-done | bytes 262160 | tf_op jit(solution)/shard_map/reduce_scatter | solution.py:122
  328.3 14.2 %all-reduce.3 = bf16[256,256]{1,0:T(8,128)(2,1)S(1)} all-reduce(f32[256,256]{1,0:T(8,128)} %reduce-scatter.8.cloned.1.call-done), channel_id=1, replica_groups=mesh['expert'=4,'mp'=2,'dp'=4] {'mp'}, use_global_device_ids=true, to_apply=%region_5.6 | all-reduce | flops 65536 | bytes 393216 | tf_op jit(solution)/shard_map/psum | solution.py:123
  342.4 1.7 convolution_bitcast_fusion
  344.1 1.8 copy.24
  345.9 1.5 convert_element_type.26
  (3 shorter events, 0.0 us)
Async XLA Ops:
  7.2 43.7 %copy-start = (bf16[2048,256]{1,0:T(8,128)(2,1)S(1)}, bf16[2048,256]{1,0:T(8,128)(2,1)}, u32[]{:S(2)}) copy-start(bf16[2048,256]{1,0:T(8,128)(2,1)} %param.10) | copy-start | bytes 3145732
  7.2 43.6 %all-gather.5.cloned.1.call-start = ((), (), s32[]{:S(2)}) async-start(), calls=%async_computation.3 | async-start | bytes 1114112 | tf_op jit(solution)/shard_map/all_gather | solution.py:108
  7.9 89.5 %all-gather.9.cloned.1.call-start = ((), (), s32[]{:S(2)}) async-start(), calls=%async_computation.5 | async-start | bytes 2228224 | tf_op jit(solution)/shard_map/all_gather | solution.py:115
  15.6 119.8 %all-gather.7.cloned.1.call-start = ((), (), s32[]{:S(2)}) async-start(), calls=%async_computation.4 | async-start | bytes 2228224 | tf_op jit(solution)/shard_map/all_gather | solution.py:111
  65.0 187.6 %reduce-scatter.4.cloned.1.call-start = ((), (), s32[]{:S(2)}) async-start(), calls=%async_computation.6 | async-start | bytes 4456448 | tf_op jit(solution)/shard_map/reduce_scatter | solution.py:120
  180.6 147.7 %reduce-scatter.8.cloned.1.call-start = ((), (), s32[]{:S(2)}) async-start(), calls=%async_computation.8 | async-start | bytes 4456448 | tf_op jit(solution)/shard_map/reduce_scatter | solution.py:122
  181.2 164.7 %reduce-scatter.6.cloned.1.call-start = ((), (), s32[]{:S(2)}) async-start(), calls=%async_computation.7 | async-start | bytes 393216 | tf_op jit(solution)/shard_map/reduce_scatter | solution.py:121
Sparse Core Ops, SparseCore 0:
  10.2 40.5 all-gather.4
  53.0 40.5 all-gather.8
  95.7 39.6 all-gather.6
  180.7 71.8 reduce-scatter.3
  256.3 71.9 reduce-scatter.7
  330.3 10.6 reduce-scatter.5
